TPU v7x, 32 devices: a whole 2x2x4 slice. The times are simulated.
32 devices in a mesh: gx: 4 (over z), gy: 8 (over y, x, core).
Axes of the slice: x: 2, y: 2, z: 4, core: 2. Of those that a mesh axis runs over, the one named last changes fastest.
Arguments:
- tables: float32 [2, 262144, 128], P(None, ('gx', 'gy')), may hold values from -0.9 to 0.9
- cold_rows: int32 [32, 2, 32, 16], P(('gx', 'gy')), may hold values from 0 to 8191, as said below
- cold_bags: int32 [32, 2, 32, 16], P(('gx', 'gy')), may hold values from -1 to 127, as said below
- hot_rows: int32 [2, 256], replicated, may hold values from 0 to 262143
- hot_ids: int32 [4096, 2, 8], P(('gx', 'gy')), may hold values from 0 to 255
Outputs:
- pooled: float32 [4096, 2, 128], P(('gx', 'gy'))
Inputs may be any that keep to these rules, and one draw needn't show every extreme that they name: `cold_rows`: every entry names one of the owner's 8192 rows. `cold_bags`: live slots of one sender, table and owner come first, the empty ones (-1) after them; in every draw each table has an owner whose 16 slots are all live from every sender.
All inputs are finite; a program needn't handle non-finite values.
Results may differ from a plain program's by a relative error of at most 0.0003.
Values sent between devices are 32-bit elements; how exact they have to be, the bound alone decides.
No kernel may reach another device: no remote copies, remote signals or barrier semaphores. Data moves between devices by JAX's collectives and lax.ppermute only.
A program may use at most 64 MiB of HBM per device.

v0:
```python
import math
import jax
import jax.numpy as jnp
from jax import lax
from jax.sharding import PartitionSpec as P


def pick_rows(table, indices):
    count = indices.shape[0]
    block = math.gcd(512, count)
    row_ids = jnp.arange(table.shape[0], dtype=jnp.int32)
    grouped = indices.reshape(count // block, block)

    def one_block(wanted):
        selector = (wanted[:, None] == row_ids[None, :]).astype(jnp.float32)
        return jnp.dot(
            selector, table, precision=lax.Precision.HIGHEST, preferred_element_type=jnp.float32
        )

    return lax.map(one_block, grouped).reshape(count, table.shape[1])


def body(tables, cold_rows, cold_bags, hot_rows, hot_ids):
    axis_x = lax.axis_size("gx")
    axis_y = lax.axis_size("gy")
    peer_count = axis_x * axis_y
    table_count, rows_dev, emb_width = tables.shape
    slot_cap = cold_rows.shape[3]
    batch_rows = hot_ids.shape[0]
    hot_count = hot_rows.shape[1]
    my_index = lax.axis_index(("gx", "gy"))
    hot_owner = hot_rows // rows_dev
    local_rows = jnp.where(hot_owner == my_index, hot_rows - my_index * rows_dev, -1)
    picked = jax.vmap(pick_rows)(tables, local_rows)
    hot_table = lax.psum(picked, ("gx", "gy"))
    matches = jnp.sum(
        (
            hot_ids[:, :, :, None] == jnp.arange(hot_count, dtype=jnp.int32)[None, None, None, :]
        ).astype(jnp.float32),
        axis=2,
    )
    hot_part = jnp.einsum("bth,thd->btd", matches, hot_table, precision=lax.Precision.HIGHEST)
    my_rows = cold_rows[0]
    my_bags = cold_bags[0]
    got_rows, got_bags = (
        lax.all_to_all(my_rows, ("gx", "gy"), split_axis=1, concat_axis=1, tiled=True),
        lax.all_to_all(my_bags, ("gx", "gy"), split_axis=1, concat_axis=1, tiled=True),
    )
    wanted_rows = jnp.where(got_bags >= 0, got_rows, -1)
    looked = jax.vmap(pick_rows)(tables, wanted_rows.reshape(table_count, -1))
    looked = looked.reshape(table_count, peer_count, slot_cap, emb_width)
    samples = jnp.arange(batch_rows, dtype=jnp.int32)
    returned = lax.all_to_all(looked, ("gx", "gy"), split_axis=1, concat_axis=1, tiled=True)
    onehot = (my_bags[:, None, :, :] == samples[None, :, None, None]).astype(jnp.float32)
    cold_part = jnp.einsum("tbpc,tpcd->btd", onehot, returned, precision=lax.Precision.HIGHEST)
    return cold_part + hot_part


def solution(mesh):
    return jax.shard_map(
        body,
        mesh=mesh,
        in_specs=(
            P(None, ("gx", "gy"), None),
            P(("gx", "gy"), None, None, None),
            P(("gx", "gy"), None, None, None),
            P(),
            P(("gx", "gy"), None, None),
        ),
        out_specs=P(("gx", "gy"), None, None),
        check_vma=False,
    )
```

profile of v0, /device:TPU:0, one launch (start us, length us, event | category | flops | bytes accessed | tf_op | source)
XLA Modules:
  0.0 203.2 jit_solution(9199264976657592994)
XLA Ops:
  6.5 1.4 copy.23
  7.9 7.3 %all-to-all-start.1 = ((s32[2,32,16]{2,0,1:T(2,128)}), s32[2,32,16]{2,0,1:T(2,128)S(1)}, u32[]{:S(2)}, u32[]{:S(2)}) async-start(s32[2,32,16]{2,0,1:T(2,128)} %bitcast.1), calls=%async_computation.1 | async-start | bytes 65536 | tf_op jit(solution)/shard_map/all_to_all | solution.py:46
  15.3 1.4 copy.22
  16.7 5.9 %all-to-all-done.1 = s32[2,32,16]{2,0,1:T(2,128)S(1)} async-done(((s32[2,32,16]{2,0,1:T(2,128)}), s32[2,32,16]{2,0,1:T(2,128)S(1)}, u32[]{:S(2)}, u32[]{:S(2)}) %all-to-all-start.1) | async-done | bytes 4128 | tf_op jit(solution)/shard_map/all_to_all | solution.py:46
  22.5 2.6 %all-to-all-start = ((s32[2,32,16]{2,0,1:T(2,128)}), s32[2,32,16]{2,0,1:T(2,128)S(1)}, u32[]{:S(2)}, u32[]{:S(2)}) async-start(s32[2,32,16]{2,0,1:T(2,128)} %bitcast), calls=%async_computation | async-start | bytes 65536 | tf_op jit(solution)/shard_map/all_to_all | solution.py:47
  25.1 7.2 %all-to-all-done = s32[2,32,16]{2,0,1:T(2,128)S(1)} async-done(((s32[2,32,16]{2,0,1:T(2,128)}), s32[2,32,16]{2,0,1:T(2,128)S(1)}, u32[]{:S(2)}, u32[]{:S(2)}) %all-to-all-start) | async-done | bytes 4128 | tf_op jit(solution)/shard_map/all_to_all | solution.py:47
  32.4 0.1 eq.74
  32.5 0.0 copy-start.1
  32.5 18.0 %fusion = f32[2,512,128]{2,1,0:T(8,128)S(1)} fusion(f32[2,8192,128]{2,1,0:T(8,128)} %param.5, s32[2,512]{1,0:T(2,128)S(1)} %eq.74), kind=kOutput, calls=%fused_computation.1 | convolution fusion | flops 12893290496 | bytes 8916992 | tf_op jit(solution)/shard_map/vmap()/while/body/eval_jaxpr/dot_general | solution.py:16
  50.5 0.0 copy-start
  50.5 0.9 copy.25
  51.4 2.6 %all-to-all-start.2 = ((f32[2,32,16,128]{3,2,0,1:T(8,128)}), f32[2,32,16,128]{3,2,0,1:T(8,128)S(1)}, u32[]{:S(2)}, u32[]{:S(2)}) async-start(f32[2,32,16,128]{3,2,0,1:T(8,128)} %copy.25), calls=%async_computation.2 | async-start | bytes 1048576 | tf_op jit(solution)/shard_map/all_to_all | solution.py:53
  54.0 0.2 all-reduce.2.cloned.1.call-start
  54.2 0.0 copy-done.1
  54.3 11.7 %fusion.2 = f32[2,256,128]{2,1,0:T(8,128)} fusion(f32[2,8192,128]{2,1,0:T(8,128)} %param.5, s32[2,256]{1,0:T(2,128)S(1)} %compare_select_fusion.1), kind=kOutput, calls=%fused_computation.4 | convolution fusion | flops 6446645248 | bytes 8652800 | tf_op jit(solution)/shard_map/vmap()/while/body/eval_jaxpr/dot_general | solution.py:16
  66.0 0.0 all-reduce.2.cloned.1.call-update
  66.0 0.0 copy-done
  66.0 0.1 copy.26
  66.2 0.8 convert_reduce_fusion
  67.0 2.6 %all-to-all-done.2 = f32[2,32,16,128]{3,2,0,1:T(8,128)S(1)} async-done(((f32[2,32,16,128]{3,2,0,1:T(8,128)}), f32[2,32,16,128]{3,2,0,1:T(8,128)S(1)}, u32[]{:S(2)}, u32[]{:S(2)}) %all-to-all-start.2) | async-done | bytes 524320 | tf_op jit(solution)/shard_map/all_to_all | solution.py:53
  69.6 1.5 convolution_bitcast_fusion
  71.1 122.8 %all-reduce.2.cloned.1.call-done = f32[2,256,128]{2,1,0:T(8,128)} async-done(((f32[2,256,128]{2,1,0:T(8,128)}), f32[2,256,128]{2,1,0:T(8,128)}) %all-reduce.2.cloned.1.call-update) | async-done | bytes 262160 | tf_op jit(solution)/shard_map/psum | solution.py:35
  194.0 1.6 fusion.4
  195.6 0.8 copy.29
  (3 shorter events, 0.0 us)
Async XLA Ops:
  7.9 14.6 %all-to-all-start.1 = ((s32[2,32,16]{2,0,1:T(2,128)}), s32[2,32,16]{2,0,1:T(2,128)S(1)}, u32[]{:S(2)}, u32[]{:S(2)}) async-start(s32[2,32,16]{2,0,1:T(2,128)} %bitcast.1), calls=%async_computation.1 | async-start | bytes 65536 | tf_op jit(solution)/shard_map/all_to_all | solution.py:46
  22.5 9.8 %all-to-all-start = ((s32[2,32,16]{2,0,1:T(2,128)}), s32[2,32,16]{2,0,1:T(2,128)S(1)}, u32[]{:S(2)}, u32[]{:S(2)}) async-start(s32[2,32,16]{2,0,1:T(2,128)} %bitcast), calls=%async_computation | async-start | bytes 65536 | tf_op jit(solution)/shard_map/all_to_all | solution.py:47
  32.5 21.8 %copy-start.1 = (s32[2,256]{1,0:T(2,128)S(1)}, s32[2,256]{1,0:T(2,128)}, u32[]{:S(2)}) copy-start(s32[2,256]{1,0:T(2,128)} %param.8) | copy-start | bytes 6148
  50.5 15.5 %copy-start = (s32[128,2,8]{0,2,1:T(8,128)S(1)}, s32[128,2,8]{0,2,1:T(8,128)}, u32[]{:S(2)}) copy-start(s32[128,2,8]{0,2,1:T(8,128)} %param.9) | copy-start | bytes 24580
  51.4 18.2 %all-to-all-start.2 = ((f32[2,32,16,128]{3,2,0,1:T(8,128)}), f32[2,32,16,128]{3,2,0,1:T(8,128)S(1)}, u32[]{:S(2)}, u32[]{:S(2)}) async-start(f32[2,32,16,128]{3,2,0,1:T(8,128)} %copy.25), calls=%async_computation.2 | async-start | bytes 1048576 | tf_op jit(solution)/shard_map/all_to_all | solution.py:53
  54.0 140.0 %all-reduce.2.cloned.1.call-start = ((), (), s32[]{:S(2)}) async-start(), calls=%async_computation.3 | async-start | bytes 524288 | tf_op jit(solution)/shard_map/psum | solution.py:35
Sparse Core Ops, SparseCore 0:
  66.1 127.7 all-reduce.1
where the time goes:
time: 204 us; the launch traced here: 203 us
  waiting for transfers between devices  139 us (68%)
  matrix products  32.8 us (16%)
  between operations  13.5 us (7%)
  starting transfers between devices  12.7 us (6%)
  local copies, waits for them, and re-layouts  4.66 us (2%)
    psum x1, waiting for transfers between devices, body(): hot_table = lax.psum(picked, ('gx', 'gy'))  123 us
    dot_general x2, matrix products, one_block(): jnp.dot(selector, table, precision=lax.Precision.HIGHEST, preferred_eleme...  29.7 us
    all_to_all x1, starting transfers between devices, body(): lax.all_to_all(my_rows, ('gx', 'gy'), split_axis=1, concat_axis=1, tiled=...  7.33 us
    all_to_all x1, waiting for transfers between devices, body(): lax.all_to_all(my_bags, ('gx', 'gy'), split_axis=1, concat_axis=1, tiled=...  7.25 us
    all_to_all x1, waiting for transfers between devices, body(): lax.all_to_all(my_rows, ('gx', 'gy'), split_axis=1, concat_axis=1, tiled=...  5.86 us
  transfers between devices with their start and end apart: 4, of which 4 were waited for; matrix products, arithmetic and copies ran while one was open for 8% of the time, Pallas kernels for 0%

commit v1 on v0

--- a/solution.py
+++ b/solution.py
@@ -32,7 +32,7 @@
     hot_owner = hot_rows // rows_dev
     local_rows = jnp.where(hot_owner == my_index, hot_rows - my_index * rows_dev, -1)
     picked = jax.vmap(pick_rows)(tables, local_rows)
-    hot_table = lax.psum(picked, ("gx", "gy"))
+    hot_table = lax.all_gather(picked, ("gx", "gy")).sum(axis=0)
     matches = jnp.sum(
         (
             hot_ids[:, :, :, None] == jnp.arange(hot_count, dtype=jnp.int32)[None, None, None, :]

time: 204 us -> 117 us (0.57)
  waiting for transfers between devices: 139 us -> 44.3 us
  blocking collectives: 0 us -> 9 us
  other arithmetic: 0.86 us -> 5.35 us
  starting transfers between devices: 12.7 us -> 9.93 us
    psum x1 -> x0, waiting for transfers between devices: 123 us -> none  [body(): hot_table = lax.psum(picked, ('gx', 'gy'))]
    all_to_all x1, waiting for transfers between devices: 2.63 us -> 24.6 us  [body(): lax.all_to_all(looked, ('gx', 'gy'), split_axis=1, concat_axis=1, tiled=T...]
    all_gather x0 -> x1, waiting for transfers between devices: none -> 12.6 us  [body(): hot_table = lax.all_gather(picked, ('gx', 'gy')).sum(axis=0)]
    all_to_all x0 -> x1, blocking collectives: none -> 9 us  [body(): lax.all_to_all(my_rows, ('gx', 'gy'), split_axis=1, concat_axis=1, tiled=...]
    all_to_all x1 -> x0, starting transfers between devices: 7.33 us -> none  [body(): lax.all_to_all(my_rows, ('gx', 'gy'), split_axis=1, concat_axis=1, tiled=...]
    all_to_all x1 -> x0, waiting for transfers between devices: 5.86 us -> none  [body(): lax.all_to_all(my_rows, ('gx', 'gy'), split_axis=1, concat_axis=1, tiled=...]
    all_to_all x1, starting transfers between devices: 2.55 us -> 7.33 us  [body(): lax.all_to_all(my_bags, ('gx', 'gy'), split_axis=1, concat_axis=1, tiled=...]
    reduce_sum x0 -> x1, other arithmetic: none -> 3.79 us  [body(): hot_table = lax.all_gather(picked, ('gx', 'gy')).sum(axis=0)]
  transfers between devices with their start and end apart: 4 -> 3, of which waited for: 4 -> 3; matrix products, arithmetic and copies ran while one was open for 8% -> 19% of each run, Pallas kernels for 0% -> 0%
where the time goes in v1:
time: 117 us
  waiting for transfers between devices  44.3 us (38%)
  matrix products  31.9 us (27%)
  between operations  13.5 us (12%)
  starting transfers between devices  9.93 us (8%)
  blocking collectives  9 us (8%)
  other arithmetic  5.35 us (5%)
  local copies, waits for them, and re-layouts  2.69 us (2%)
    dot_general x2, matrix products, one_block(): jnp.dot(selector, table, precision=lax.Precision.HIGHEST, preferred_eleme...  29.7 us
    all_to_all x1, waiting for transfers between devices, body(): lax.all_to_all(looked, ('gx', 'gy'), split_axis=1, concat_axis=1, tiled=T...  24.6 us
    all_gather x1, waiting for transfers between devices, body(): hot_table = lax.all_gather(picked, ('gx', 'gy')).sum(axis=0)  12.6 us
    all_to_all x1, blocking collectives, body(): lax.all_to_all(my_rows, ('gx', 'gy'), split_axis=1, concat_axis=1, tiled=...  9 us
    all_to_all x1, starting transfers between devices, body(): lax.all_to_all(my_bags, ('gx', 'gy'), split_axis=1, concat_axis=1, tiled=...  7.33 us
    all_to_all x1, waiting for transfers between devices, body(): lax.all_to_all(my_bags, ('gx', 'gy'), split_axis=1, concat_axis=1, tiled=...  7.17 us
    reduce_sum x1, other arithmetic, body(): hot_table = lax.all_gather(picked, ('gx', 'gy')).sum(axis=0)  3.79 us
    all_to_all x1, starting transfers between devices, body(): lax.all_to_all(looked, ('gx', 'gy'), split_axis=1, concat_axis=1, tiled=T...  2.6 us
  transfers between devices with their start and end apart: 3, of which 3 were waited for; matrix products, arithmetic and copies ran while one was open for 19% of the time, Pallas kernels for 0%

profile of v1, /device:TPU:0, one launch (start us, length us, event | category | flops | bytes accessed | tf_op | source)
XLA Modules:
  0.0 116.7 jit_solution(8866116060832862002)
XLA Ops:
  6.5 0.0 all-gather.3.cloned.1.call-start
  6.5 0.7 compare_select_fusion.1
  7.3 11.7 %fusion.2 = f32[2,256,128]{2,1,0:T(8,128)} fusion(f32[2,8192,128]{2,1,0:T(8,128)} %param.5, s32[2,256]{1,0:T(2,128)S(1)} %compare_select_fusion.1), kind=kOutput, calls=%fused_computation.4 | convolution fusion | flops 6446645248 | bytes 8652800 | tf_op jit(solution)/shard_map/vmap()/while/body/eval_jaxpr/dot_general | solution.py:16
  19.0 0.0 all-gather.3.cloned.1.call-update
  19.0 0.0 copy-done
  19.0 0.7 copy.22
  19.7 7.3 %all-to-all-start = ((s32[2,32,16]{2,0,1:T(2,128)}), s32[2,32,16]{2,0,1:T(2,128)S(1)}, u32[]{:S(2)}, u32[]{:S(2)}) async-start(s32[2,32,16]{2,0,1:T(2,128)} %bitcast), calls=%async_computation | async-start | bytes 65536 | tf_op jit(solution)/shard_map/all_to_all | solution.py:47
  27.0 0.0 copy-done.1
  27.0 0.1 copy.23
  27.1 7.2 %all-to-all-done = s32[2,32,16]{2,0,1:T(2,128)S(1)} async-done(((s32[2,32,16]{2,0,1:T(2,128)}), s32[2,32,16]{2,0,1:T(2,128)S(1)}, u32[]{:S(2)}, u32[]{:S(2)}) %all-to-all-start) | async-done | bytes 4128 | tf_op jit(solution)/shard_map/all_to_all | solution.py:47
  34.3 9.0 %all_to_all.15 = s32[2,32,16]{2,0,1:T(2,128)S(1)} all-to-all(s32[2,32,16]{2,0,1:T(2,128)S(1)} %bitcast.14), channel_id=1, replica_groups=mesh['gx'=4,'gy'=8] {'gx','gy'}, dimensions={1} | all-to-all | bytes 8192 | tf_op jit(solution)/shard_map/all_to_all | solution.py:46
  43.3 0.1 eq.74
  43.4 0.0 copy-start.2
  43.4 18.0 %fusion = f32[2,512,128]{2,1,0:T(8,128)S(1)} fusion(f32[2,8192,128]{2,1,0:T(8,128)} %param.5, s32[2,512]{1,0:T(2,128)S(1)} %eq.74), kind=kOutput, calls=%fused_computation.1 | convolution fusion | flops 12893290496 | bytes 8916992 | tf_op jit(solution)/shard_map/vmap()/while/body/eval_jaxpr/dot_general | solution.py:16
  61.5 0.9 copy.25
  62.4 2.6 %all-to-all-start.2 = ((f32[2,32,16,128]{3,2,0,1:T(8,128)}), f32[2,32,16,128]{3,2,0,1:T(8,128)S(1)}, u32[]{:S(2)}, u32[]{:S(2)}) async-start(f32[2,32,16,128]{3,2,0,1:T(8,128)} %copy.25), calls=%async_computation.2 | async-start | bytes 1048576 | tf_op jit(solution)/shard_map/all_to_all | solution.py:53
  65.0 0.1 copy.26
  65.1 0.8 convert_reduce_fusion
  66.0 24.6 %all-to-all-done.2 = f32[2,32,16,128]{3,2,0,1:T(8,128)S(1)} async-done(((f32[2,32,16,128]{3,2,0,1:T(8,128)}), f32[2,32,16,128]{3,2,0,1:T(8,128)S(1)}, u32[]{:S(2)}, u32[]{:S(2)}) %all-to-all-start.2) | async-done | bytes 524320 | tf_op jit(solution)/shard_map/all_to_all | solution.py:53
  90.6 1.5 %convolution_bitcast_fusion = f32[2,128,128]{2,1,0:T(8,128)S(1)} fusion(f32[2,32,16,128]{3,2,0,1:T(8,128)S(1)} %all-to-all-done.2, s32[2,32,16]{2,0,1:T(2,128)} %bitcast), kind=kOutput, calls=%fused_computation.10 | convolution fusion | flops 201457664 | bytes 659456 | tf_op jit(solution)/shard_map/tbpc,tpcd->btd/dot_general | solution.py:55
  92.1 12.6 %all-gather.3.cloned.1.call-done = f32[64,256,128]{2,1,0:T(8,128)} async-done(((f32[2,256,128]{2,1,0:T(8,128)}), f32[64,256,128]{2,1,0:T(8,128)}) %all-gather.3.cloned.1.call-update) | async-done | bytes 8388624 | tf_op jit(solution)/shard_map/all_gather | solution.py:35
  104.6 3.8 %reduce_sum.18 = f32[2,256,128]{2,1,0:T(8,128)S(1)} reduce(f32[32,2,256,128]{3,2,1,0:T(8,128)} %bitcast.12, f32[]{:T(128)} %constant.49.clone.1), dimensions={0}, to_apply=%region_0.1 | reduce | flops 2031616 | bytes 8650756 | tf_op jit(solution)/shard_map/reduce_sum | solution.py:35
  108.4 0.6 fusion.4
  109.1 0.8 copy.29
  (5 shorter events, 0.0 us)
Async XLA Ops:
  6.5 12.5 %copy-start = (s32[1,2,32,16]{2,3,1,0:T(8,128)S(1)}, s32[1,2,32,16]{2,3,1,0:T(8,128)}, u32[]{:S(2)}) copy-start(s32[1,2,32,16]{2,3,1,0:T(8,128)} %param.7) | copy-start | bytes 12292
  6.5 20.5 %copy-start.1 = (s32[1,2,32,16]{2,3,1,0:T(8,128)S(1)}, s32[1,2,32,16]{2,3,1,0:T(8,128)}, u32[]{:S(2)}) copy-start(s32[1,2,32,16]{2,3,1,0:T(8,128)} %param.6) | copy-start | bytes 12292
  6.5 98.1 %all-gather.3.cloned.1.call-start = ((), (), s32[]{:S(2)}) async-start(), calls=%async_computation.3 | async-start | bytes 8650752 | tf_op jit(solution)/shard_map/all_gather | solution.py:35
  19.7 14.6 %all-to-all-start = ((s32[2,32,16]{2,0,1:T(2,128)}), s32[2,32,16]{2,0,1:T(2,128)S(1)}, u32[]{:S(2)}, u32[]{:S(2)}) async-start(s32[2,32,16]{2,0,1:T(2,128)} %bitcast), calls=%async_computation | async-start | bytes 65536 | tf_op jit(solution)/shard_map/all_to_all | solution.py:47
  43.4 21.6 %copy-start.2 = (s32[128,2,8]{0,2,1:T(8,128)S(1)}, s32[128,2,8]{0,2,1:T(8,128)}, u32[]{:S(2)}) copy-start(s32[128,2,8]{0,2,1:T(8,128)} %param.9) | copy-start | bytes 24580
  62.4 28.2 %all-to-all-start.2 = ((f32[2,32,16,128]{3,2,0,1:T(8,128)}), f32[2,32,16,128]{3,2,0,1:T(8,128)S(1)}, u32[]{:S(2)}, u32[]{:S(2)}) async-start(f32[2,32,16,128]{3,2,0,1:T(8,128)} %copy.25), calls=%async_computation.2 | async-start | bytes 1048576 | tf_op jit(solution)/shard_map/all_to_all | solution.py:53
Sparse Core Ops, SparseCore 0:
  19.1 85.4 all-gather.2
